TPU v7x, 32 devices: a whole 2x2x4 slice. The times are simulated.
32 devices in a mesh: pix: 8 (over z, y), rep: 4 (over x, core).
Axes of the slice: x: 2, y: 2, z: 4, core: 2. Of those that a mesh axis runs over, the one named last changes fastest.
Arguments:
- interferograms: float32 [256, 131072], P(('pix', 'rep')), may hold values from -6 to 6
- epoch_pairs: int32 [2, 256], replicated, may hold values from 0 to 63, as said below
- los: float32 [3, 131072], P(None, ('pix', 'rep')), may hold values from 0.3 to 1
- patch_place: int32 [2, 4096], replicated, may hold values from 0 to 255, as said below
- patch_depth: int32 [4096], replicated, may hold values from 0 to 7
Outputs:
- predicted: float32 [64, 131072], P(None, ('pix', 'rep'))
- slip: float32 [64, 4096], P(None, ('pix', 'rep'))
Inputs may be any that keep to these rules, and one draw needn't show every extreme that they name: `epoch_pairs`: row 0 holds an interferogram's earlier epoch and row 1 its later one; the two always differ. `patch_place`: row 0 is an east cell below 256; row 1 is a north cell below 32.
All inputs are finite; a program needn't handle non-finite values.
Results may differ from a plain program's by a relative error of at most 0.0037.
Values may be sent and summed in bfloat16 or wider, within the bound.
A program may use at most 64 MiB of HBM per device.

v0:
```python
import jax
import jax.numpy as jnp
from jax import lax
from jax.sharding import PartitionSpec as P

NEP = 64
IMG_W = 1024
pixel_step = 0.1
patch_step = 0.4
damping = 0.5
depth_base = 0.5
depth_step = 0.25


def sbas_inverse(epoch_pairs, epochs_count):
    epochs = lax.iota(jnp.int32, epochs_count)
    design = (epochs[None, :] == epoch_pairs[1][:, None]).astype(jnp.float32) - (
        epochs[None, :] == epoch_pairs[0][:, None]
    ).astype(jnp.float32)
    normal = jnp.dot(design.T, design, precision=lax.Precision.HIGHEST) + damping * jnp.eye(
        epochs_count, dtype=jnp.float32
    )
    factor = jnp.linalg.cholesky(normal)
    return jax.scipy.linalg.cho_solve((factor, True), design.T)


def green_tile(pixel, los_rows, patch_place, patch_depth):
    column = (pixel % IMG_W).astype(jnp.float32)
    line = (pixel // IMG_W).astype(jnp.float32)
    xpos = (column + 0.5) * pixel_step
    ypos = (line + 0.5) * pixel_step
    patch_x = (patch_place[0].astype(jnp.float32) + 0.5) * patch_step
    patch_y = (patch_place[1].astype(jnp.float32) + 0.5) * patch_step
    patch_z = depth_base + depth_step * patch_depth.astype(jnp.float32)
    delta_x = xpos[:, None] - patch_x[None, :]
    delta_y = ypos[:, None] - patch_y[None, :]
    delta_z = patch_z[None, :]
    dist_sq = delta_x * delta_x + delta_y * delta_y + delta_z * delta_z
    toward = (
        los_rows[0][:, None] * delta_x
        + los_rows[1][:, None] * delta_y
        + los_rows[2][:, None] * delta_z
    )
    return (delta_z * toward / (dist_sq * jnp.sqrt(dist_sq))).astype(jnp.bfloat16)


def on_device(interferograms, epoch_pairs, los, patch_place, patch_depth):
    devices = lax.axis_size(("pix", "rep"))
    ifg_dev, total = interferograms.shape
    pix_dev = total // devices
    epochs_count = NEP
    npatch = patch_depth.shape[0]
    own = npatch // devices
    pseudo = sbas_inverse(epoch_pairs, epochs_count)
    pieces = interferograms.reshape(ifg_dev, devices, pix_dev)
    series = jnp.dot(
        pseudo,
        lax.all_to_all(pieces, ("pix", "rep"), split_axis=1, concat_axis=0, tiled=True)[:, 0, :],
        precision=lax.Precision.HIGHEST,
        preferred_element_type=jnp.float32,
    )
    anchor = lax.axis_index(("pix", "rep")) * pix_dev
    width = min(512, pix_dev)
    count = pix_dev // width

    def tile_at(index):
        start = index * width
        pixel = anchor + start + lax.iota(jnp.int32, width)
        los_rows = lax.dynamic_slice_in_dim(los, start, width, 1)
        return (green_tile(pixel, los_rows, patch_place, patch_depth), start)

    def first_step(index, carry):
        rhs, bound = carry
        tile, start = tile_at(index)
        resid = lax.dynamic_slice_in_dim(series, start, width, 1).astype(jnp.bfloat16)
        rhs = rhs + jnp.dot(resid, tile, preferred_element_type=jnp.float32)
        magnitude = jnp.abs(tile)
        weight = jnp.sum(magnitude.astype(jnp.float32), axis=1).astype(jnp.bfloat16)
        bound = bound + jnp.dot(weight[None, :], magnitude, preferred_element_type=jnp.float32)
        return (rhs, bound)

    zero_rhs = jnp.zeros((epochs_count, npatch), jnp.float32)
    zero_bound = jnp.zeros((1, npatch), jnp.float32)
    rhs, bound = lax.fori_loop(0, count, first_step, (zero_rhs, zero_bound))
    rhs_all, bound_all = lax.psum((rhs, bound), ("pix", "rep"))
    slip_all = rhs_all / bound_all
    sweep_slip_half = slip_all.astype(jnp.bfloat16)

    def sweep_step(index, rhs_now):
        tile, start = tile_at(index)
        guess = lax.dot_general(
            sweep_slip_half, tile, (((1,), (1,)), ((), ())), preferred_element_type=jnp.float32
        )
        resid = (lax.dynamic_slice_in_dim(series, start, width, 1) - guess).astype(jnp.bfloat16)
        return rhs_now + jnp.dot(resid, tile, preferred_element_type=jnp.float32)

    rhs = lax.fori_loop(0, count, sweep_step, zero_rhs)
    slip_all = slip_all + lax.psum(rhs, ("pix", "rep")) / bound_all
    slip_half = slip_all.astype(jnp.bfloat16)
    slip_own = lax.dynamic_slice_in_dim(slip_all, lax.axis_index(("pix", "rep")) * own, own, 1)

    def final_step(index, predicted):
        tile, start = tile_at(index)
        block = lax.dot_general(
            slip_half, tile, (((1,), (1,)), ((), ())), preferred_element_type=jnp.float32
        )
        return lax.dynamic_update_slice_in_dim(predicted, block, start, 1)

    predicted = lax.fori_loop(0, count, final_step, jnp.zeros((epochs_count, pix_dev), jnp.float32))
    return (predicted, slip_own)


def solution(mesh):
    placed = (P(("pix", "rep"), None), P(), P(None, ("pix", "rep")), P(), P())
    return jax.shard_map(
        on_device,
        mesh=mesh,
        in_specs=placed,
        out_specs=(P(None, ("pix", "rep")), P(None, ("pix", "rep"))),
        check_vma=False,
    )
```

profile of v0, /device:TPU:0, one launch (start us, length us, event | category | flops | bytes accessed | tf_op | source)
XLA Modules:
  0.0 731.8 jit_solution(1607313868562399574)
XLA Ops:
  7.2 7.5 %all-to-all-start = ((f32[8,32,4096]{2,0,1:T(8,128)}), f32[8,32,4096]{2,0,1:T(8,128)}, u32[]{:S(2)}, u32[]{:S(2)}) async-start(f32[8,32,4096]{2,0,1:T(8,128)} %bitcast.110), calls=%async_computation | async-start | bytes 8388608 | tf_op jit(solution)/shard_map/all_to_all | solution.py:58
  28.2 80.2 %all-to-all-done = f32[8,32,4096]{2,0,1:T(8,128)} async-done(((f32[8,32,4096]{2,0,1:T(8,128)}), f32[8,32,4096]{2,0,1:T(8,128)}, u32[]{:S(2)}, u32[]{:S(2)}) %all-to-all-start) | async-done | bytes 4194336 | tf_op jit(solution)/shard_map/all_to_all | solution.py:58
  114.1 168.4 %while.53 = (s32[]{:T(128)}, f32[64,4096]{1,0:T(8,128)S(1)}, f32[1,4096]{1,0:T(1,128)S(1)}, bf16[64,4096]{1,0:T(8,128)(2,1)S(1)}, f32[1,4096]{1,0:T(1,128)S(1)},...) while((s32[]{:T(128)}, f32[64,4096]{1,0:T(8,128)S(1)}, ...), condition=%wide.region_4.5_spmd.clone, body=%wide.region_2.4_spmd.clone.sunk | while | flops 373867008 | bytes 2590974 | solution.py:84
  121.9 6.8 abs_reduce_fusion.2
  142.8 6.8 abs_reduce_fusion.2
  163.8 6.8 abs_reduce_fusion.2
  184.8 6.8 abs_reduce_fusion.2
  205.8 6.8 abs_reduce_fusion.2
  226.8 6.8 abs_reduce_fusion.2
  247.7 6.8 abs_reduce_fusion.2
  268.7 6.8 abs_reduce_fusion.2
  283.6 38.4 %psum.22 = f32[4096]{0:T(1024)S(1)} all-reduce(f32[4096]{0:T(1024)S(1)} %bitcast.147), channel_id=1, replica_groups=mesh['pix'=8,'rep'=4] {'pix','rep'}, use_global_device_ids=true, to_apply=%region_6.7 | all-reduce | flops 4096 | bytes 32768 | tf_op jit(solution)/shard_map/psum | solution.py:85
  322.0 92.1 %all-reduce.3.cloned.1.call-done = f32[64,4096]{1,0:T(8,128)} async-done(((f32[64,4096]{1,0:T(8,128)}), f32[64,4096]{1,0:T(8,128)}) %all-reduce.3.cloned.1.call-update) | async-done | bytes 1048592 | tf_op jit(solution)/shard_map/psum | solution.py:85
  415.4 117.2 %while.54 = (s32[]{:T(128)}, f32[64,4096]{1,0:T(8,128)S(1)}, f32[64,4096]{1,0:T(8,128)}, f32[1,4096]{1,0:T(1,128)S(1)}, f32[3,4096]{1,0:T(4,128)}, /*index=5*/s3...) while((s32[]{:T(128)}, f32[64,4096]{1,0:T(8,128)S(1)}, ...), condition=%wide.region_8.9_spmd.clone, body=%wide.region_7.8_spmd.clone.sunk | while | flops 600417280 | bytes 3068157 | solution.py:97
  416.4 13.6 %convolution_add_fusion.8 = f32[64,4096]{1,0:T(8,128)S(1)} fusion(f32[4096]{0:T(1024)S(1)} %mul.1511, f32[512]{0:T(512)S(1)} %bitcast.143, f32[4096]{0:T(1024)S(1)} %bitcast.128, f32[512]{0:T(512)S(1)} %get-tuple-element.1055, f32[512]{0:T(512)S(1)} %bitcast.142, f32[4096]{0:T(1024)S(1)} %bitcast.129, f32[512]{0:T(512)S(1)} %get-tuple-element.1058, ...), kind=kOutput, calls=%fused_computation.86.clone.1 | convolution fusion | flops 600375296 | bytes 2904069 | tf_op jit(solution)/shard_map/while/body/eval_jaxpr/dot_general | solution.py:95
  431.0 13.6 %convolution_add_fusion.8 = f32[64,4096]{1,0:T(8,128)S(1)} fusion(f32[4096]{0:T(1024)S(1)} %mul.1511, f32[512]{0:T(512)S(1)} %bitcast.143, f32[4096]{0:T(1024)S(1)} %bitcast.128, f32[512]{0:T(512)S(1)} %get-tuple-element.1055, f32[512]{0:T(512)S(1)} %bitcast.142, f32[4096]{0:T(1024)S(1)} %bitcast.129, f32[512]{0:T(512)S(1)} %get-tuple-element.1058, ...), kind=kOutput, calls=%fused_computation.86.clone.1 | convolution fusion | flops 600375296 | bytes 2904069 | tf_op jit(solution)/shard_map/while/body/eval_jaxpr/dot_general | solution.py:95
  445.6 13.6 %convolution_add_fusion.8 = f32[64,4096]{1,0:T(8,128)S(1)} fusion(f32[4096]{0:T(1024)S(1)} %mul.1511, f32[512]{0:T(512)S(1)} %bitcast.143, f32[4096]{0:T(1024)S(1)} %bitcast.128, f32[512]{0:T(512)S(1)} %get-tuple-element.1055, f32[512]{0:T(512)S(1)} %bitcast.142, f32[4096]{0:T(1024)S(1)} %bitcast.129, f32[512]{0:T(512)S(1)} %get-tuple-element.1058, ...), kind=kOutput, calls=%fused_computation.86.clone.1 | convolution fusion | flops 600375296 | bytes 2904069 | tf_op jit(solution)/shard_map/while/body/eval_jaxpr/dot_general | solution.py:95
  460.3 13.6 %convolution_add_fusion.8 = f32[64,4096]{1,0:T(8,128)S(1)} fusion(f32[4096]{0:T(1024)S(1)} %mul.1511, f32[512]{0:T(512)S(1)} %bitcast.143, f32[4096]{0:T(1024)S(1)} %bitcast.128, f32[512]{0:T(512)S(1)} %get-tuple-element.1055, f32[512]{0:T(512)S(1)} %bitcast.142, f32[4096]{0:T(1024)S(1)} %bitcast.129, f32[512]{0:T(512)S(1)} %get-tuple-element.1058, ...), kind=kOutput, calls=%fused_computation.86.clone.1 | convolution fusion | flops 600375296 | bytes 2904069 | tf_op jit(solution)/shard_map/while/body/eval_jaxpr/dot_general | solution.py:95
  474.9 13.6 %convolution_add_fusion.8 = f32[64,4096]{1,0:T(8,128)S(1)} fusion(f32[4096]{0:T(1024)S(1)} %mul.1511, f32[512]{0:T(512)S(1)} %bitcast.143, f32[4096]{0:T(1024)S(1)} %bitcast.128, f32[512]{0:T(512)S(1)} %get-tuple-element.1055, f32[512]{0:T(512)S(1)} %bitcast.142, f32[4096]{0:T(1024)S(1)} %bitcast.129, f32[512]{0:T(512)S(1)} %get-tuple-element.1058, ...), kind=kOutput, calls=%fused_computation.86.clone.1 | convolution fusion | flops 600375296 | bytes 2904069 | tf_op jit(solution)/shard_map/while/body/eval_jaxpr/dot_general | solution.py:95
  489.5 13.6 %convolution_add_fusion.8 = f32[64,4096]{1,0:T(8,128)S(1)} fusion(f32[4096]{0:T(1024)S(1)} %mul.1511, f32[512]{0:T(512)S(1)} %bitcast.143, f32[4096]{0:T(1024)S(1)} %bitcast.128, f32[512]{0:T(512)S(1)} %get-tuple-element.1055, f32[512]{0:T(512)S(1)} %bitcast.142, f32[4096]{0:T(1024)S(1)} %bitcast.129, f32[512]{0:T(512)S(1)} %get-tuple-element.1058, ...), kind=kOutput, calls=%fused_computation.86.clone.1 | convolution fusion | flops 600375296 | bytes 2904069 | tf_op jit(solution)/shard_map/while/body/eval_jaxpr/dot_general | solution.py:95
  504.1 13.6 %convolution_add_fusion.8 = f32[64,4096]{1,0:T(8,128)S(1)} fusion(f32[4096]{0:T(1024)S(1)} %mul.1511, f32[512]{0:T(512)S(1)} %bitcast.143, f32[4096]{0:T(1024)S(1)} %bitcast.128, f32[512]{0:T(512)S(1)} %get-tuple-element.1055, f32[512]{0:T(512)S(1)} %bitcast.142, f32[4096]{0:T(1024)S(1)} %bitcast.129, f32[512]{0:T(512)S(1)} %get-tuple-element.1058, ...), kind=kOutput, calls=%fused_computation.86.clone.1 | convolution fusion | flops 600375296 | bytes 2904069 | tf_op jit(solution)/shard_map/while/body/eval_jaxpr/dot_general | solution.py:95
  518.8 13.6 %convolution_add_fusion.8 = f32[64,4096]{1,0:T(8,128)S(1)} fusion(f32[4096]{0:T(1024)S(1)} %mul.1511, f32[512]{0:T(512)S(1)} %bitcast.143, f32[4096]{0:T(1024)S(1)} %bitcast.128, f32[512]{0:T(512)S(1)} %get-tuple-element.1055, f32[512]{0:T(512)S(1)} %bitcast.142, f32[4096]{0:T(1024)S(1)} %bitcast.129, f32[512]{0:T(512)S(1)} %get-tuple-element.1058, ...), kind=kOutput, calls=%fused_computation.86.clone.1 | convolution fusion | flops 600375296 | bytes 2904069 | tf_op jit(solution)/shard_map/while/body/eval_jaxpr/dot_general | solution.py:95
  533.5 129.8 %all-reduce.5.cloned.1.call-done = f32[64,4096]{1,0:T(8,128)} async-done(((f32[64,4096]{1,0:T(8,128)}), f32[64,4096]{1,0:T(8,128)}) %all-reduce.5.cloned.1.call-update) | async-done | bytes 1048592 | tf_op jit(solution)/shard_map/psum | solution.py:98
  664.8 59.0 %while.52 = (s32[]{:T(128)}, f32[64,4096]{1,0:T(8,128)S(1)}, f32[1,4096]{1,0:T(1,128)S(1)}, f32[3,4096]{1,0:T(4,128)}, s32[]{:T(128)}, /*index=5*/f32[1,4096]{1,...) while((s32[]{:T(128)}, f32[64,4096]{1,0:T(8,128)S(1)}, ...), condition=%wide.region_11.12_spmd, body=%wide.region_10.11_spmd.sunk | while | flops 299934720 | bytes 895211 | solution.py:109
  (193 shorter events, 204.1 us)
Async XLA Ops:
  7.2 7.6 %copy-start.7 = (s32[2,256]{1,0:T(2,128)S(1)}, s32[2,256]{1,0:T(2,128)}, u32[]{:S(2)}) copy-start(s32[2,256]{1,0:T(2,128)} %param.12) | copy-start | bytes 6148
  7.2 20.3 %copy-start.6 = (s32[4096]{0:T(1024)S(1)}, s32[4096]{0:T(1024)}, u32[]{:S(2)}) copy-start(s32[4096]{0:T(1024)} %param.15) | copy-start | bytes 49156
  7.2 20.9 %copy-start.5 = (s32[2,4096]{1,0:T(2,128)S(1)}, s32[2,4096]{1,0:T(2,128)}, u32[]{:S(2)}) copy-start(s32[2,4096]{1,0:T(2,128)} %param.14) | copy-start | bytes 98308
  7.2 101.2 %all-to-all-start = ((f32[8,32,4096]{2,0,1:T(8,128)}), f32[8,32,4096]{2,0,1:T(8,128)}, u32[]{:S(2)}, u32[]{:S(2)}) async-start(f32[8,32,4096]{2,0,1:T(8,128)} %bitcast.110), calls=%async_computation | async-start | bytes 8388608 | tf_op jit(solution)/shard_map/all_to_all | solution.py:58
  14.7 399.4 %all-reduce.3.cloned.1.call-start = ((), (), s32[]{:S(2)}) async-start(), calls=%async_computation.1 | async-start | bytes 2097152 | tf_op jit(solution)/shard_map/psum | solution.py:85
  282.5 1.0 copy-start.1
  283.5 379.8 %all-reduce.5.cloned.1.call-start = ((), (), s32[]{:S(2)}) async-start(), calls=%async_computation.2 | async-start | bytes 2097152 | tf_op jit(solution)/shard_map/psum | solution.py:98
  322.0 93.4 %copy-start.4 = (f32[4096]{0:T(1024)}, f32[4096]{0:T(1024)S(1)}, u32[]{:S(2)}) copy-start(f32[4096]{0:T(1024)S(1)} %psum.22) | copy-start | bytes 49156
  415.4 248.0 %copy-start = (f32[64,4096]{1,0:T(8,128)S(1)}, f32[64,4096]{1,0:T(8,128)}, u32[]{:S(2)}) copy-start(f32[64,4096]{1,0:T(8,128)} %all-reduce.3.cloned.1.call-done) | copy-start | bytes 3145732
  532.5 1.0 copy-start.2
  723.8 1.0 copy-start.3
Sparse Core Ops, SparseCore 0:
  283.7 130.3 all-reduce.2
  533.7 129.6 all-reduce.4
where the time goes:
time: 738 us; the launch traced here: 732 us
  waiting for transfers between devices  302 us (41%)
  matrix products  271 us (37%)
  other arithmetic  71.6 us (10%)
  blocking collectives  38.4 us (5%)
  local copies, waits for them, and re-layouts  24.6 us (3%)
  between operations  14.5 us (2%)
  starting transfers between devices  7.54 us (1%)
    psum x1, waiting for transfers between devices, on_device(): slip_all = slip_all + lax.psum(rhs, ('pix', 'rep')) / bound_all  130 us
    dot_general x8, matrix products, sweep_step(): return rhs_now + jnp.dot(resid, tile, preferred_element_type=jnp.float32)  109 us
    psum x1, waiting for transfers between devices, on_device(): rhs_all, bound_all = lax.psum((rhs, bound), ('pix', 'rep'))  92.1 us
    all_to_all x1, waiting for transfers between devices, on_device(): lax.all_to_all(pieces, ('pix', 'rep'), split_axis=1, concat_axis=0, tiled...  80.2 us
    reduce_sum x8, other arithmetic, first_step(): weight = jnp.sum(magnitude.astype(jnp.float32), axis=1).astype(jnp.bfloat16)  54.8 us
    dot_general x8, matrix products, first_step(): rhs = rhs + jnp.dot(resid, tile, preferred_element_type=jnp.float32)  52.5 us
    dot_general x8, matrix products, first_step(): jnp.dot(weight[None, :], magnitude, preferred_element_type=jnp.float32)  52.4 us
    dot_general x8, matrix products, final_step(): lax.dot_general(slip_half, tile, (((1,), (1,)), ((), ())), preferred_elem...  50.8 us
  transfers between devices with their start and end apart: 3, of which 3 were waited for; matrix products, arithmetic and copies ran while one was open for 2% of the time, Pallas kernels for 0%

commit v1 on v0

--- a/solution.py
+++ b/solution.py
@@ -10,6 +10,12 @@
 damping = 0.5
 depth_base = 0.5
 depth_step = 0.25
+
+
+def add_all(shard, axis):
+    parts = lax.all_gather(shard, axis, axis=0, tiled=False)
+    total = parts.sum(axis=0)
+    return total
 
 
 def sbas_inverse(epoch_pairs, epochs_count):
@@ -95,7 +101,7 @@
         return rhs_now + jnp.dot(resid, tile, preferred_element_type=jnp.float32)
 
     rhs = lax.fori_loop(0, count, sweep_step, zero_rhs)
-    slip_all = slip_all + lax.psum(rhs, ("pix", "rep")) / bound_all
+    slip_all = slip_all + add_all(rhs, ("pix", "rep")) / bound_all
     slip_half = slip_all.astype(jnp.bfloat16)
     slip_own = lax.dynamic_slice_in_dim(slip_all, lax.axis_index(("pix", "rep")) * own, own, 1)
 

time: 738 us -> 821 us (1.11)
  waiting for transfers between devices: 302 us -> 366 us
  other arithmetic: 71.6 us -> 83 us
  matrix products: 271 us -> 280 us
    all_gather x0 -> x1, waiting for transfers between devices: none -> 193 us  [add_all(): parts = lax.all_gather(shard, axis, axis=0, tiled=False)]
    psum x1 -> x0, waiting for transfers between devices: 130 us -> none  [on_device(): slip_all = slip_all + lax.psum(rhs, ('pix', 'rep')) / bound_all]
    reduce_sum x0 -> x1, other arithmetic: none -> 11.9 us  [add_all(): total = parts.sum(axis=0)]
    dot_general x8, matrix products: 50.8 us -> 59.1 us  [final_step(): lax.dot_general(slip_half, tile, (((1,), (1,)), ((), ())), preferred_elem...]
where the time goes in v1:
time: 821 us; the launch traced here: 815 us
  waiting for transfers between devices  366 us (45%)
  matrix products  280 us (34%)
  other arithmetic  83 us (10%)
  blocking collectives  38.4 us (5%)
  local copies, waits for them, and re-layouts  24.6 us (3%)
  between operations  14.5 us (2%)
    all_gather x1, waiting for transfers between devices, add_all(): parts = lax.all_gather(shard, axis, axis=0, tiled=False)  193 us
    dot_general x8, matrix products, sweep_step(): return rhs_now + jnp.dot(resid, tile, preferred_element_type=jnp.float32)  109 us
    psum x1, waiting for transfers between devices, on_device(): rhs_all, bound_all = lax.psum((rhs, bound), ('pix', 'rep'))  92.1 us
    all_to_all x1, waiting for transfers between devices, on_device(): lax.all_to_all(pieces, ('pix', 'rep'), split_axis=1, concat_axis=0, tiled...  80.2 us
    dot_general x8, matrix products, final_step(): lax.dot_general(slip_half, tile, (((1,), (1,)), ((), ())), preferred_elem...  59.1 us
    reduce_sum x8, other arithmetic, first_step(): weight = jnp.sum(magnitude.astype(jnp.float32), axis=1).astype(jnp.bfloat16)  54.8 us
    dot_general x8, matrix products, first_step(): rhs = rhs + jnp.dot(resid, tile, preferred_element_type=jnp.float32)  52.5 us
    dot_general x8, matrix products, first_step(): jnp.dot(weight[None, :], magnitude, preferred_element_type=jnp.float32)  52.4 us
  transfers between devices with their start and end apart: 3, of which 3 were waited for; matrix products, arithmetic and copies ran while one was open for 2% of the time, Pallas kernels for 0%

profile of v1, /device:TPU:0, one launch (start us, length us, event | category | flops | bytes accessed | tf_op | source)
XLA Modules:
  0.0 815.1 jit_solution(7307088277148498381)
XLA Ops:
  7.2 7.5 all-to-all-start
  28.2 80.2 %all-to-all-done = f32[8,32,4096]{2,0,1:T(8,128)} async-done(((f32[8,32,4096]{2,0,1:T(8,128)}), f32[8,32,4096]{2,0,1:T(8,128)}, u32[]{:S(2)}, u32[]{:S(2)}) %all-to-all-start) | async-done | bytes 4194336 | tf_op jit(solution)/shard_map/all_to_all | solution.py:64
  114.1 168.4 %while.53 = (s32[]{:T(128)}, f32[64,4096]{1,0:T(8,128)S(1)}, f32[1,4096]{1,0:T(1,128)S(1)}, bf16[64,4096]{1,0:T(8,128)(2,1)S(1)}, f32[1,4096]{1,0:T(1,128)S(1)},...) while((s32[]{:T(128)}, f32[64,4096]{1,0:T(8,128)S(1)}, ...), condition=%wide.region_4.5_spmd.clone, body=%wide.region_2.4_spmd.clone.sunk | while | flops 373867008 | bytes 2590974 | solution.py:90
  283.6 38.4 %psum.15 = f32[4096]{0:T(1024)S(1)} all-reduce(f32[4096]{0:T(1024)S(1)} %bitcast.149), channel_id=1, replica_groups=mesh['pix'=8,'rep'=4] {'pix','rep'}, use_global_device_ids=true, to_apply=%region_6.7 | all-reduce | flops 4096 | bytes 32768 | tf_op jit(solution)/shard_map/psum | solution.py:91
  322.0 92.1 %all-reduce.2.cloned.1.call-done = f32[64,4096]{1,0:T(8,128)} async-done(((f32[64,4096]{1,0:T(8,128)}), f32[64,4096]{1,0:T(8,128)}) %all-reduce.2.cloned.1.call-update) | async-done | bytes 1048592 | tf_op jit(solution)/shard_map/psum | solution.py:91
  415.4 117.2 %while.54 = (s32[]{:T(128)}, f32[64,4096]{1,0:T(8,128)S(1)}, f32[64,4096]{1,0:T(8,128)}, f32[1,4096]{1,0:T(1,128)S(1)}, f32[3,4096]{1,0:T(4,128)}, /*index=5*/s3...) while((s32[]{:T(128)}, f32[64,4096]{1,0:T(8,128)S(1)}, ...), condition=%wide.region_8.9_spmd.clone, body=%wide.region_7.8_spmd.clone.sunk | while | flops 600417280 | bytes 3068157 | solution.py:103
  416.4 13.6 %convolution_add_fusion.8 = f32[64,4096]{1,0:T(8,128)S(1)} fusion(f32[4096]{0:T(1024)S(1)} %mul.1511, f32[512]{0:T(512)S(1)} %bitcast.145, f32[4096]{0:T(1024)S(1)} %bitcast.130, f32[512]{0:T(512)S(1)} %get-tuple-element.1055, f32[512]{0:T(512)S(1)} %bitcast.144, f32[4096]{0:T(1024)S(1)} %bitcast.131, f32[512]{0:T(512)S(1)} %get-tuple-element.1058, ...), kind=kOutput, calls=%fused_computation.86.clone.1 | convolution fusion | flops 600375296 | bytes 2904069 | tf_op jit(solution)/shard_map/while/body/eval_jaxpr/dot_general | solution.py:101
  431.0 13.6 %convolution_add_fusion.8 = f32[64,4096]{1,0:T(8,128)S(1)} fusion(f32[4096]{0:T(1024)S(1)} %mul.1511, f32[512]{0:T(512)S(1)} %bitcast.145, f32[4096]{0:T(1024)S(1)} %bitcast.130, f32[512]{0:T(512)S(1)} %get-tuple-element.1055, f32[512]{0:T(512)S(1)} %bitcast.144, f32[4096]{0:T(1024)S(1)} %bitcast.131, f32[512]{0:T(512)S(1)} %get-tuple-element.1058, ...), kind=kOutput, calls=%fused_computation.86.clone.1 | convolution fusion | flops 600375296 | bytes 2904069 | tf_op jit(solution)/shard_map/while/body/eval_jaxpr/dot_general | solution.py:101
  445.7 13.6 %convolution_add_fusion.8 = f32[64,4096]{1,0:T(8,128)S(1)} fusion(f32[4096]{0:T(1024)S(1)} %mul.1511, f32[512]{0:T(512)S(1)} %bitcast.145, f32[4096]{0:T(1024)S(1)} %bitcast.130, f32[512]{0:T(512)S(1)} %get-tuple-element.1055, f32[512]{0:T(512)S(1)} %bitcast.144, f32[4096]{0:T(1024)S(1)} %bitcast.131, f32[512]{0:T(512)S(1)} %get-tuple-element.1058, ...), kind=kOutput, calls=%fused_computation.86.clone.1 | convolution fusion | flops 600375296 | bytes 2904069 | tf_op jit(solution)/shard_map/while/body/eval_jaxpr/dot_general | solution.py:101
  460.3 13.6 %convolution_add_fusion.8 = f32[64,4096]{1,0:T(8,128)S(1)} fusion(f32[4096]{0:T(1024)S(1)} %mul.1511, f32[512]{0:T(512)S(1)} %bitcast.145, f32[4096]{0:T(1024)S(1)} %bitcast.130, f32[512]{0:T(512)S(1)} %get-tuple-element.1055, f32[512]{0:T(512)S(1)} %bitcast.144, f32[4096]{0:T(1024)S(1)} %bitcast.131, f32[512]{0:T(512)S(1)} %get-tuple-element.1058, ...), kind=kOutput, calls=%fused_computation.86.clone.1 | convolution fusion | flops 600375296 | bytes 2904069 | tf_op jit(solution)/shard_map/while/body/eval_jaxpr/dot_general | solution.py:101
  474.9 13.6 %convolution_add_fusion.8 = f32[64,4096]{1,0:T(8,128)S(1)} fusion(f32[4096]{0:T(1024)S(1)} %mul.1511, f32[512]{0:T(512)S(1)} %bitcast.145, f32[4096]{0:T(1024)S(1)} %bitcast.130, f32[512]{0:T(512)S(1)} %get-tuple-element.1055, f32[512]{0:T(512)S(1)} %bitcast.144, f32[4096]{0:T(1024)S(1)} %bitcast.131, f32[512]{0:T(512)S(1)} %get-tuple-element.1058, ...), kind=kOutput, calls=%fused_computation.86.clone.1 | convolution fusion | flops 600375296 | bytes 2904069 | tf_op jit(solution)/shard_map/while/body/eval_jaxpr/dot_general | solution.py:101
  489.5 13.6 %convolution_add_fusion.8 = f32[64,4096]{1,0:T(8,128)S(1)} fusion(f32[4096]{0:T(1024)S(1)} %mul.1511, f32[512]{0:T(512)S(1)} %bitcast.145, f32[4096]{0:T(1024)S(1)} %bitcast.130, f32[512]{0:T(512)S(1)} %get-tuple-element.1055, f32[512]{0:T(512)S(1)} %bitcast.144, f32[4096]{0:T(1024)S(1)} %bitcast.131, f32[512]{0:T(512)S(1)} %get-tuple-element.1058, ...), kind=kOutput, calls=%fused_computation.86.clone.1 | convolution fusion | flops 600375296 | bytes 2904069 | tf_op jit(solution)/shard_map/while/body/eval_jaxpr/dot_general | solution.py:101
  504.2 13.6 %convolution_add_fusion.8 = f32[64,4096]{1,0:T(8,128)S(1)} fusion(f32[4096]{0:T(1024)S(1)} %mul.1511, f32[512]{0:T(512)S(1)} %bitcast.145, f32[4096]{0:T(1024)S(1)} %bitcast.130, f32[512]{0:T(512)S(1)} %get-tuple-element.1055, f32[512]{0:T(512)S(1)} %bitcast.144, f32[4096]{0:T(1024)S(1)} %bitcast.131, f32[512]{0:T(512)S(1)} %get-tuple-element.1058, ...), kind=kOutput, calls=%fused_computation.86.clone.1 | convolution fusion | flops 600375296 | bytes 2904069 | tf_op jit(solution)/shard_map/while/body/eval_jaxpr/dot_general | solution.py:101
  518.8 13.6 %convolution_add_fusion.8 = f32[64,4096]{1,0:T(8,128)S(1)} fusion(f32[4096]{0:T(1024)S(1)} %mul.1511, f32[512]{0:T(512)S(1)} %bitcast.145, f32[4096]{0:T(1024)S(1)} %bitcast.130, f32[512]{0:T(512)S(1)} %get-tuple-element.1055, f32[512]{0:T(512)S(1)} %bitcast.144, f32[4096]{0:T(1024)S(1)} %bitcast.131, f32[512]{0:T(512)S(1)} %get-tuple-element.1058, ...), kind=kOutput, calls=%fused_computation.86.clone.1 | convolution fusion | flops 600375296 | bytes 2904069 | tf_op jit(solution)/shard_map/while/body/eval_jaxpr/dot_general | solution.py:101
  533.6 193.3 %all-gather.3.cloned.1.call-done = f32[2048,4096]{1,0:T(8,128)} async-done(((f32[64,4096]{1,0:T(8,128)}), f32[2048,4096]{1,0:T(8,128)}) %all-gather.3.cloned.1.call-update) | async-done | bytes 33554448 | tf_op jit(solution)/shard_map/all_gather | solution.py:16
  726.8 11.9 %reduce_sum.23 = f32[64,4096]{1,0:T(8,128)S(1)} reduce(f32[32,64,4096]{2,1,0:T(8,128)} %bitcast.110, f32[]{:T(128)} %constant.489.clone.1), dimensions={0}, to_apply=%region_9.10 | reduce | flops 8126464 | bytes 34603012 | tf_op jit(solution)/shard_map/reduce_sum | solution.py:17
  739.8 67.3 %while.52 = (s32[]{:T(128)}, f32[64,4096]{1,0:T(8,128)S(1)}, f32[1,4096]{1,0:T(1,128)S(1)}, f32[3,4096]{1,0:T(4,128)}, s32[]{:T(128)}, /*index=5*/f32[1,4096]{1,...) while((s32[]{:T(128)}, f32[64,4096]{1,0:T(8,128)S(1)}, ...), condition=%wide.region_11.12_spmd, body=%wide.region_10.11_spmd.sunk | while | flops 299934720 | bytes 895211 | solution.py:115
  740.8 7.4 fusion.114
  757.6 7.4 fusion.114
  766.0 7.4 fusion.114
  774.4 7.4 fusion.114
  782.9 7.4 fusion.114
  791.3 7.4 fusion.114
  799.7 7.4 fusion.114
  (196 shorter events, 215.0 us)
Async XLA Ops:
  7.2 7.6 copy-start.8
  7.2 20.3 %copy-start.7 = (s32[4096]{0:T(1024)S(1)}, s32[4096]{0:T(1024)}, u32[]{:S(2)}) copy-start(s32[4096]{0:T(1024)} %param.15) | copy-start | bytes 49156
  7.2 20.9 %copy-start.6 = (s32[2,4096]{1,0:T(2,128)S(1)}, s32[2,4096]{1,0:T(2,128)}, u32[]{:S(2)}) copy-start(s32[2,4096]{1,0:T(2,128)} %param.14) | copy-start | bytes 98308
  7.2 101.2 %all-to-all-start = ((f32[8,32,4096]{2,0,1:T(8,128)}), f32[8,32,4096]{2,0,1:T(8,128)}, u32[]{:S(2)}, u32[]{:S(2)}) async-start(f32[8,32,4096]{2,0,1:T(8,128)} %bitcast.112), calls=%async_computation | async-start | bytes 8388608 | tf_op jit(solution)/shard_map/all_to_all | solution.py:64
  14.7 399.4 %all-reduce.2.cloned.1.call-start = ((), (), s32[]{:S(2)}) async-start(), calls=%async_computation.1 | async-start | bytes 2097152 | tf_op jit(solution)/shard_map/psum | solution.py:91
  282.5 1.0 copy-start.1
  283.5 443.3 %all-gather.3.cloned.1.call-start = ((), (), s32[]{:S(2)}) async-start(), calls=%async_computation.2 | async-start | bytes 34603008 | tf_op jit(solution)/shard_map/all_gather | solution.py:16
  321.9 93.4 %copy-start.4 = (f32[4096]{0:T(1024)}, f32[4096]{0:T(1024)S(1)}, u32[]{:S(2)}) copy-start(f32[4096]{0:T(1024)S(1)} %psum.15) | copy-start | bytes 49156
  532.6 1.0 copy-start.2
  726.8 11.9 %copy-start = (f32[64,4096]{1,0:T(8,128)S(1)}, f32[64,4096]{1,0:T(8,128)}, u32[]{:S(2)}) copy-start(f32[64,4096]{1,0:T(8,128)} %all-reduce.2.cloned.1.call-done) | copy-start | bytes 3145732
  726.8 11.9 %copy-start.5 = (f32[4096]{0:T(1024)S(1)}, f32[4096]{0:T(1024)}, u32[]{:S(2)}) copy-start(f32[4096]{0:T(1024)} %copy-done.4) | copy-start | bytes 49156
  807.1 1.0 copy-start.3
Sparse Core Ops, SparseCore 0:
  283.6 130.3 all-reduce.1
  533.7 193.1 all-gather.2
